TPU v7x, 256 devices: a whole 4x4x8 slice. The times are simulated.
256 devices in a mesh: rep: 2 (over core), tab: 128 (over y, z, x).
Axes of the slice: x: 4, y: 4, z: 8, core: 2. Of those that a mesh axis runs over, the one named last changes fastest.
Arguments:
- grad_out: bfloat16 [65536, 128, 128], P(('rep', 'tab')), may hold values from -1.5 to 1.5
- indices: int32 [128, 65536], P('tab', 'rep'), may hold values from 0 to 1023
- projections: bfloat16 [128, 128, 128], P('tab'), may hold values from -0.75 to 0.75
- widths: int32 [128], replicated, may hold values from 16 to 128
- hot_ids: int32 [128, 32], P('tab'), may hold values from 0 to 1023, as said below
Outputs:
- cold_grad: float32 [2, 128, 1024, 128], P('rep', 'tab')
- hot_grad: float32 [128, 32, 128], P('tab', 'rep')
Inputs may be any that keep to these rules, and one draw needn't show every extreme that they name: `hot_ids`: the 32 hot rows of one table are distinct.
All inputs are finite; a program needn't handle non-finite values.
Results may differ from a plain program's by a relative error of at most 0.005.
Values may be sent and summed in bfloat16 or wider, within the bound.
A program may use at most 128 MiB of HBM per device.

v0:
```python
import math

import jax
import jax.numpy as jnp
from jax import lax
from jax.sharding import PartitionSpec as P

ROWS = 1024


def swapped(block, axis, bit):
    count = lax.axis_size(axis)
    route = []
    for low in range(count):
        high = low | 1 << bit
        if high != low and high < count:
            route += [(low, high), (high, low)]
    return lax.ppermute(block, axis, route)


def block_sums(narrow_rows, lookups):
    total_len = narrow_rows.shape[0]
    block_len = math.gcd(total_len, 4096)
    turn_count = total_len // block_len
    positions = lax.broadcasted_iota(jnp.int32, (1, ROWS), 1)

    def add_block(block, totals):
        piece_rows = lax.dynamic_slice_in_dim(narrow_rows, block * block_len, block_len, 0)
        row_ids = lax.dynamic_slice_in_dim(lookups, block * block_len, block_len, 0)
        onehot = (row_ids[:, None] == positions).astype(jnp.bfloat16)
        return totals + lax.dot_general(
            onehot, piece_rows, (((0,), (0,)), ((), ())), preferred_element_type=jnp.float32
        )

    start_sums = jnp.zeros((ROWS, narrow_rows.shape[1]), jnp.float32)
    return lax.fori_loop(0, turn_count, add_block, start_sums)


def shards(grad_out, indices, projections, widths, hot_ids):
    tab_dev = projections.shape[0]
    base_width = projections.shape[2]
    columns = lax.broadcasted_iota(jnp.int32, (1, 1, base_width), 2)
    first_table = lax.axis_index("tab") * tab_dev
    own_widths = lax.dynamic_slice_in_dim(widths, first_table, tab_dev, 0)
    received = lax.all_to_all(grad_out, "tab", split_axis=1, concat_axis=0, tiled=True)
    full_proj = jnp.einsum(
        "bte,tej->tbj", received, projections, preferred_element_type=jnp.float32
    )
    narrow = jnp.where(columns < own_widths[:, None, None], full_proj, 0.0).astype(jnp.bfloat16)
    table_grads = [block_sums(narrow[0], indices[0])]
    row_grads = jnp.stack(table_grads)
    own_hot = jnp.take_along_axis(row_grads, hot_ids[:, :, None], axis=1)
    half_hot = hot_ids.shape[1] // 2
    replica = lax.axis_index("rep")
    kept_rows = lax.dynamic_slice_in_dim(own_hot, replica * half_hot, half_hot, 1)
    given_rows = lax.dynamic_slice_in_dim(own_hot, (1 - replica) * half_hot, half_hot, 1)
    partner = swapped(given_rows, "rep", 0)
    hot_grad = kept_rows + partner
    all_rows = lax.broadcasted_iota(jnp.int32, (1, 1, ROWS), 2)
    is_hot = jnp.any(hot_ids[:, :, None] == all_rows, axis=1)
    cold_grad = jnp.where(is_hot[:, :, None], jnp.float32(0.0), row_grads)
    return (cold_grad[None], hot_grad)


def solution(mesh):
    placed = (
        P(("rep", "tab"), None, None),
        P("tab", "rep"),
        P("tab", None, None),
        P(),
        P("tab", None),
    )
    return jax.shard_map(
        shards,
        mesh=mesh,
        in_specs=placed,
        out_specs=(P("rep", "tab", None, None), P("tab", "rep", None)),
        check_vma=False,
    )
```

profile of v0, /device:TPU:1, one launch (start us, length us, event | category | flops | bytes accessed | tf_op | source)
XLA Modules:
  0.0 287.0 jit_solution(2860464138068047582)
XLA Ops:
  0.6 0.0 copy-start
  0.6 12.0 %copy.8 = bf16[256,128,128]{2,0,1:T(8,128)(2,1)} copy(bf16[256,128,128]{2,1,0:T(8,128)(2,1)} %param.7) | data formatting | bytes 16777216 | tf_op args[0]
  12.6 17.2 %all-to-all-start = ((bf16[256,128,128]{2,0,1:T(8,128)(2,1)}), bf16[256,128,128]{2,0,1:T(8,128)(2,1)}, u32[]{:S(2)}, u32[]{:S(2)}) async-start(bf16[256,128,128]{2,0,1:T(8,128)(2,1)} %copy.8), calls=%async_computation | async-start | bytes 16777216 | tf_op jit(solution)/shard_map/all_to_all | solution.py:45
  29.8 0.0 copy-done.1
  29.9 0.6 dynamic_slice.23
  30.4 0.6 iota_compare_fusion.5
  31.1 0.1 fusion.8
  31.2 180.6 %all-to-all-done = bf16[256,128,128]{2,0,1:T(8,128)(2,1)} async-done(((bf16[256,128,128]{2,0,1:T(8,128)(2,1)}), bf16[256,128,128]{2,0,1:T(8,128)(2,1)}, u32[]{:S(2)}, u32[]{:S(2)}) %all-to-all-start) | async-done | bytes 8388640 | tf_op jit(solution)/shard_map/all_to_all | solution.py:45
  211.8 8.9 %fusion.7 = bf16[32768,128]{1,0:T(8,128)(2,1)} fusion(bf16[32768,128]{1,0:T(8,128)(2,1)} %bitcast.5, pred[128]{0:T(512)(128)(4,1)S(1)} %iota_compare_fusion.5, bf16[1,128,128]{2,1,0:T(8,128)(2,1)S(1)} %copy-done), kind=kOutput, calls=%fused_computation.9 | convolution fusion | flops 1082130432 | bytes 16810112 | tf_op jit(solution)/shard_map/bte,tej->tbj/dot_general | solution.py:46
  220.8 57.6 %while.14 = (s32[]{:T(128)}, f32[1024,128]{1,0:T(8,128)S(1)}, s32[32768]{0:T(1024)}, bf16[32768,128]{1,0:T(8,128)(2,1)}, s32[]{:T(128)}, /*index=5*/s32[]{:T(128)}, s32[]{:T(128)}, s32[]{:T(128)}) while((s32[]{:T(128)}, f32[1024,128]{1,0:T(8,128)S(1)}, s32[32768]{0:T(1024)}, bf16[32768,128]{1,0:T(8,128)(2,1)}, s32[]{:T(128)}, ...), condition=%wide.region_2.3_spmd.clone, body=%wide.region_1.2_spmd.clone.sunk | while | flops 1078198272 | bytes 2146453 | solution.py:36
  220.8 0.7 dynamic_slice.35
  221.5 6.5 %fusion.15 = f32[1024,128]{1,0:T(8,128)S(1)} fusion(s32[4096]{0:T(1024)S(1)} %dynamic_slice.35, bf16[32768,128]{1,0:T(8,128)(2,1)} %get-tuple-element.166, s32[]{:T(128)S(6)} %select_n.81, f32[1024,128]{1,0:T(8,128)S(1)} %get-tuple-element.156, pred[]{:T(512)S(6)} %compare.3), kind=kOutput, calls=%fused_computation.5.clone.1 | convolution fusion | flops 1078198272 | bytes 2113541 | tf_op jit(solution)/shard_map/while/body/eval_jaxpr/dot_general | solution.py:31
  228.0 0.7 dynamic_slice.35
  228.7 6.5 %fusion.15 = f32[1024,128]{1,0:T(8,128)S(1)} fusion(s32[4096]{0:T(1024)S(1)} %dynamic_slice.35, bf16[32768,128]{1,0:T(8,128)(2,1)} %get-tuple-element.166, s32[]{:T(128)S(6)} %select_n.81, f32[1024,128]{1,0:T(8,128)S(1)} %get-tuple-element.156, pred[]{:T(512)S(6)} %compare.3), kind=kOutput, calls=%fused_computation.5.clone.1 | convolution fusion | flops 1078198272 | bytes 2113541 | tf_op jit(solution)/shard_map/while/body/eval_jaxpr/dot_general | solution.py:31
  235.2 0.7 dynamic_slice.35
  235.9 6.5 %fusion.15 = f32[1024,128]{1,0:T(8,128)S(1)} fusion(s32[4096]{0:T(1024)S(1)} %dynamic_slice.35, bf16[32768,128]{1,0:T(8,128)(2,1)} %get-tuple-element.166, s32[]{:T(128)S(6)} %select_n.81, f32[1024,128]{1,0:T(8,128)S(1)} %get-tuple-element.156, pred[]{:T(512)S(6)} %compare.3), kind=kOutput, calls=%fused_computation.5.clone.1 | convolution fusion | flops 1078198272 | bytes 2113541 | tf_op jit(solution)/shard_map/while/body/eval_jaxpr/dot_general | solution.py:31
  242.4 0.7 dynamic_slice.35
  243.1 6.5 %fusion.15 = f32[1024,128]{1,0:T(8,128)S(1)} fusion(s32[4096]{0:T(1024)S(1)} %dynamic_slice.35, bf16[32768,128]{1,0:T(8,128)(2,1)} %get-tuple-element.166, s32[]{:T(128)S(6)} %select_n.81, f32[1024,128]{1,0:T(8,128)S(1)} %get-tuple-element.156, pred[]{:T(512)S(6)} %compare.3), kind=kOutput, calls=%fused_computation.5.clone.1 | convolution fusion | flops 1078198272 | bytes 2113541 | tf_op jit(solution)/shard_map/while/body/eval_jaxpr/dot_general | solution.py:31
  249.6 0.7 dynamic_slice.35
  250.3 6.5 %fusion.15 = f32[1024,128]{1,0:T(8,128)S(1)} fusion(s32[4096]{0:T(1024)S(1)} %dynamic_slice.35, bf16[32768,128]{1,0:T(8,128)(2,1)} %get-tuple-element.166, s32[]{:T(128)S(6)} %select_n.81, f32[1024,128]{1,0:T(8,128)S(1)} %get-tuple-element.156, pred[]{:T(512)S(6)} %compare.3), kind=kOutput, calls=%fused_computation.5.clone.1 | convolution fusion | flops 1078198272 | bytes 2113541 | tf_op jit(solution)/shard_map/while/body/eval_jaxpr/dot_general | solution.py:31
  256.8 0.7 dynamic_slice.35
  257.5 6.5 %fusion.15 = f32[1024,128]{1,0:T(8,128)S(1)} fusion(s32[4096]{0:T(1024)S(1)} %dynamic_slice.35, bf16[32768,128]{1,0:T(8,128)(2,1)} %get-tuple-element.166, s32[]{:T(128)S(6)} %select_n.81, f32[1024,128]{1,0:T(8,128)S(1)} %get-tuple-element.156, pred[]{:T(512)S(6)} %compare.3), kind=kOutput, calls=%fused_computation.5.clone.1 | convolution fusion | flops 1078198272 | bytes 2113541 | tf_op jit(solution)/shard_map/while/body/eval_jaxpr/dot_general | solution.py:31
  264.0 0.7 dynamic_slice.35
  264.7 6.5 %fusion.15 = f32[1024,128]{1,0:T(8,128)S(1)} fusion(s32[4096]{0:T(1024)S(1)} %dynamic_slice.35, bf16[32768,128]{1,0:T(8,128)(2,1)} %get-tuple-element.166, s32[]{:T(128)S(6)} %select_n.81, f32[1024,128]{1,0:T(8,128)S(1)} %get-tuple-element.156, pred[]{:T(512)S(6)} %compare.3), kind=kOutput, calls=%fused_computation.5.clone.1 | convolution fusion | flops 1078198272 | bytes 2113541 | tf_op jit(solution)/shard_map/while/body/eval_jaxpr/dot_general | solution.py:31
  271.2 0.7 dynamic_slice.35
  272.0 6.5 %fusion.15 = f32[1024,128]{1,0:T(8,128)S(1)} fusion(s32[4096]{0:T(1024)S(1)} %dynamic_slice.35, bf16[32768,128]{1,0:T(8,128)(2,1)} %get-tuple-element.166, s32[]{:T(128)S(6)} %select_n.81, f32[1024,128]{1,0:T(8,128)S(1)} %get-tuple-element.156, pred[]{:T(512)S(6)} %compare.3), kind=kOutput, calls=%fused_computation.5.clone.1 | convolution fusion | flops 1078198272 | bytes 2113541 | tf_op jit(solution)/shard_map/while/body/eval_jaxpr/dot_general | solution.py:31
  278.4 0.6 gather_fusion
  279.0 0.1 bitcast_select_fusion
  279.1 6.3 %collective-permute-start = (f32[1,16,128]{2,1,0:T(8,128)S(1)}, f32[1,16,128]{2,1,0:T(8,128)S(1)}, u32[]{:S(2)}, u32[]{:S(2)}) collective-permute-start(f32[1,16,128]{2,1,0:T(8,128)S(1)} %constant_dynamic-slice_fusion), channel_id=1, source_target_pairs={{0,128},{128,0},{1,129},{129,1},{2,130},{130,2},{3,131},{131,3},{4... | collective-permute-start | bytes 24584 | tf_op jit(solution)/shard_map/ppermute | solution.py:18
  285.4 1.0 select_bitcast_fusion
  286.4 0.0 collective-permute-done
  286.4 0.6 dynamic-slice_add_fusion
  (9 shorter events, 0.0 us)
Async XLA Ops:
  0.6 211.2 %copy-start = (bf16[1,128,128]{2,1,0:T(8,128)(2,1)S(1)}, bf16[1,128,128]{2,1,0:T(8,128)(2,1)}, u32[]{:S(2)}) copy-start(bf16[1,128,128]{2,1,0:T(8,128)(2,1)} %param.9) | copy-start | bytes 98308
  12.6 17.2 %copy-start.1 = (s32[128]{0:T(128)S(1)}, s32[128]{0:T(128)}, u32[]{:S(2)}) copy-start(s32[128]{0:T(128)} %param.10) | copy-start | bytes 1540
  12.6 18.5 %copy-start.2 = (s32[1,32]{1,0:T(1,128)S(1)}, s32[1,32]{1,0:T(1,128)}, u32[]{:S(2)}) copy-start(s32[1,32]{1,0:T(1,128)} %param.11) | copy-start | bytes 388
  12.6 199.2 %all-to-all-start = ((bf16[256,128,128]{2,0,1:T(8,128)(2,1)}), bf16[256,128,128]{2,0,1:T(8,128)(2,1)}, u32[]{:S(2)}, u32[]{:S(2)}) async-start(bf16[256,128,128]{2,0,1:T(8,128)(2,1)} %copy.8), calls=%async_computation | async-start | bytes 16777216 | tf_op jit(solution)/shard_map/all_to_all | solution.py:45
  279.1 7.3 %collective-permute-start = (f32[1,16,128]{2,1,0:T(8,128)S(1)}, f32[1,16,128]{2,1,0:T(8,128)S(1)}, u32[]{:S(2)}, u32[]{:S(2)}) collective-permute-start(f32[1,16,128]{2,1,0:T(8,128)S(1)} %constant_dynamic-slice_fusion), channel_id=1, source_target_pairs={{0,128},{128,0},{1,129},{129,1},{2,130},{130,2},{3,131},{131,3},{4... | collective-permute-start | bytes 24584 | tf_op jit(solution)/shard_map/ppermute | solution.py:18
where the time goes:
time: 288 us; the launch traced here: 287 us
  waiting for transfers between devices  181 us (63%)
  matrix products  60.6 us (21%)
  starting transfers between devices  23.5 us (8%)
  local copies, waits for them, and re-layouts  19 us (7%)
    all_to_all x1, waiting for transfers between devices, shards(): lax.all_to_all(grad_out, 'tab', split_axis=1, concat_axis=0, tiled=True)  181 us
    dot_general x8, matrix products, add_block(): lax.dot_general(onehot, piece_rows, (((0,), (0,)), ((), ())), preferred_e...  51.7 us
    all_to_all x1, starting transfers between devices, shards(): lax.all_to_all(grad_out, 'tab', split_axis=1, concat_axis=0, tiled=True)  17.2 us
    unnamed x7, local copies, waits for them, and re-layouts  12 us
    dot_general x1, matrix products, shards(): jnp.einsum('bte,tej->tbj', received, projections, preferred_element_type=...  8.93 us
    ppermute x1, starting transfers between devices, swapped(): return lax.ppermute(block, axis, route)  6.28 us
    dynamic_slice x8, local copies, waits for them, and re-layouts, add_block(): row_ids = lax.dynamic_slice_in_dim(lookups, block * block_len, block_len, 0)  5.78 us
  transfers between devices with their start and end apart: 2, of which 1 were waited for; matrix products, arithmetic and copies ran while one was open for 1% of the time, Pallas kernels for 0%

commit v1 on v0

v1 whole, which is shorter than its diff:
```python
import jax
import jax.numpy as jnp
from jax import lax
from jax.experimental import pallas as pl
from jax.experimental.pallas import tpu as pltpu
from jax.sharding import PartitionSpec as P

ROWS = 1024
NX, NY, NZ = 4, 4, 8
STEPS = 4
F32 = jnp.float32
BF16 = jnp.bfloat16


def kernel(grad_ref, idx_ref, proj_ref, widths_ref, hot_ref, cold_ref, hotout_ref,
           stage, tmp, turn, raw, fsum, own, part, leaf, near, zsend, zrecv,
           zi, pi, hot_all, hot_got,
           load_sem, raw_s, raw_r, leaf_s, leaf_r, near_s, near_r, z_s, z_r,
           iz_s, iz_r, iq_s, iq_r, hot_s, hot_r):
    rep = lax.axis_index("rep")
    tab = lax.axis_index("tab")
    x = tab % NX
    z = (tab // NX) % NZ
    y = tab // (NX * NZ)

    def at(px, py, pz):
        return {"tab": (py * NZ + pz) * NX + px}

    def peer(mode, along, shift):
        on_y = (1 - along) * (1 - mode) + along * mode
        return at((x + (1 - on_y) * shift) % NX, (y + on_y * shift) % NY, z)

    def remote(src, dst, s, r, dev):
        return pltpu.make_async_remote_copy(
            src_ref=src, dst_ref=dst, send_sem=s, recv_sem=r,
            device_id=dev, device_id_type=pl.DeviceIdType.MESH)

    def pair_of(step):
        return (z // 2 + 2 + 3 * step + (step // 2) * (3 - 2 * (step % 2))) % 4

    def load(step, d):
        tile = ((y + d) % NY) * 4 + pair_of(step)
        return pltpu.make_async_copy(
            grad_ref.at[:, pl.ds(pl.multiple_of(tile * 8, 8), 8), :],
            stage.at[step, d], load_sem.at[step, d])

    def start_loads(i, c):
        load(i // 4, i % 4).start()
        return c

    lax.fori_loop(0, 16, start_loads, 0)

    barrier = pltpu.get_barrier_semaphore()

    def greet(dev):
        pl.semaphore_signal(barrier, inc=1, device_id=dev, device_id_type=pl.DeviceIdType.MESH)

    for d in range(1, 4):
        greet(at((x + d) % NX, y, z))
        greet(at(x, (y + d) % NY, z))
    for d in range(1, 8):
        greet(at(x, y, (z + d) % NZ))
    greet({"rep": 1 - rep})
    pl.semaphore_wait(barrier, 14)

    def iz(d):
        to = (z + d) % NZ
        return remote(idx_ref.at[to], zi.at[z % 2, z // 2], iz_s.at[d - 1], iz_r.at[d - 1], at(x, y, to))

    for d in range(1, 8):
        iz(d).start()
    zi[z % 2, z // 2] = idx_ref[z]

    def raw_copy(mode, step, d):
        pos = y * (1 - mode) + x * mode
        return remote(turn.at[mode, step, (pos + d) % 4], raw.at[mode, step, d - 1],
                      raw_s.at[mode, step, d - 1], raw_r.at[mode, step, d - 1], peer(mode, 0, d))

    def relayout(step):
        def one(d, c):
            load(step, d).wait()
            tmp[...] = stage[step, d].astype(F32).reshape(2048, 128)
            to_y = (y + d) % NY
            for px in range(4):
                turn[0, step, to_y, px] = tmp[pl.ds(px, 256, stride=8), :].astype(BF16)
            for px in range(4):
                turn[1, step, px, to_y] = tmp[pl.ds(4 + px, 256, stride=8), :].astype(BF16)
            return c

        lax.fori_loop(0, 4, one, 0)

        def send(i, c):
            raw_copy(i % 2, step, i // 2 + 1).start()
            return c

        lax.fori_loop(0, 6, send, 0)

    relayout(0)

    def iq(mode, d):
        pos = x * (1 - mode) + y * mode
        return remote(zi.at[mode, :, (pos + d) % 4], pi.at[mode, :, pos],
                      iq_s.at[mode, d - 1], iq_r.at[mode, d - 1], peer(mode, 1, d))

    for d in range(1, 8):
        iz(d).wait()
    for mode in range(2):
        for d in range(1, 4):
            iq(mode, d).start()
    pi[0, :, x] = zi[0, :, x]
    pi[1, :, y] = zi[1, :, y]
    for mode in range(2):
        for d in range(1, 4):
            iq(mode, d).wait()

    rows = lax.broadcasted_iota(jnp.int32, (ROWS, 128), 0)

    def onehot(ids, src):
        halves = []
        for h in range(2):
            line = pi[ids + (pl.ds(2 * src + h, 1), slice(None))]
            halves.append(jnp.where(rows == line, F32(1), F32(0)).astype(BF16))
        return jnp.concatenate(halves, axis=1)

    def table_sum(mode, step, dest):
        pos = y * (1 - mode) + x * mode
        ids = (mode, pair_of(step), dest)
        fsum[...] = jnp.dot(onehot(ids, pos), turn[mode, step, pos, dest], preferred_element_type=F32)

        def other(d, c):
            src = (pos + 4 - d) % 4
            fsum[...] += jnp.dot(onehot(ids, src), raw[mode, step, d - 1, dest], preferred_element_type=F32)
            return c

        lax.fori_loop(1, 4, other, 0)

    HALF = ROWS // 2

    def leaf_copy(mode, step, side):
        return remote(part.at[mode, step, 0, pl.ds(side * HALF, HALF)], leaf.at[mode, step, side],
                      leaf_s.at[mode, step, side], leaf_r.at[mode, step, side], peer(mode, 1, 1 + 2 * side))

    def near_copy(mode, step, side):
        return remote(part.at[mode, step, 1 + side], near.at[mode, step, side],
                      near_s.at[mode, step, side], near_r.at[mode, step, side], peer(mode, 1, 1 + 2 * side))

    def z_copy(mode, step):
        to = pair_of(step) * 2 + mode
        return remote(zsend.at[mode, step], zrecv.at[z], z_s.at[mode, step], z_r.at[z], at(x, y, to))

    def z_arrival(src):
        return remote(zsend.at[0, 0], zrecv.at[src], z_s.at[0, 0], z_r.at[src], at(x, y, src))

    def step_body(step, c):
        @pl.when(step < STEPS - 1)
        def _():
            relayout(step + 1)

        def arrive(i, c):
            raw_copy(i % 2, step, i // 2 + 1).wait_recv()
            return c

        lax.fori_loop(0, 6, arrive, 0)

        def table(i, c):
            mode = i % 2
            j = i // 2
            pos = x * (1 - mode) + y * mode
            shift = (2 + 2 * j + 3 * (j // 2)) % 4
            table_sum(mode, step, (pos + shift) % 4)

            @pl.when(j == 0)
            def _():
                part[mode, step, 0] = fsum[...].astype(BF16)
                leaf_copy(mode, step, 0).start()
                leaf_copy(mode, step, 1).start()

            @pl.when(j == 1)
            def _():
                own[mode, step] = fsum[...]

            @pl.when(j >= 2)
            def _():
                side = j - 2
                leaf_copy(mode, step, side).wait_recv()
                at_row = pl.multiple_of(side * HALF, HALF)
                fsum[pl.ds(at_row, HALF), :] += leaf[mode, step, side].astype(F32)
                part[mode, step, 1 + side] = fsum[...].astype(BF16)
                near_copy(mode, step, side).start()

            return c

        lax.fori_loop(0, 8, table, 0)

        @pl.when(step > 0)
        def _():
            finish(step - 1)

        return c

    def finish(step):
        def one(mode, c):
            near_copy(mode, step, 0).wait_recv()
            near_copy(mode, step, 1).wait_recv()
            zsend[mode, step] = (own[mode, step] + near[mode, step, 0].astype(F32)
                                 + near[mode, step, 1].astype(F32)).astype(BF16)

            @pl.when(pair_of(step) * 2 + mode - z != 0)
            def _():
                z_copy(mode, step).start()

            return c

        lax.fori_loop(0, 2, one, 0)

    lax.fori_loop(0, STEPS, step_body, 0)
    finish(STEPS - 1)

    fsum[...] = zsend[z % 2, STEPS - 1].astype(F32)

    def gather_z(d, c):
        src = (z + d) % NZ
        z_arrival(src).wait_recv()
        fsum[...] += zrecv[src].astype(F32)
        return c

    lax.fori_loop(1, 8, gather_z, 0)

    total = fsum[...]
    high = total.astype(BF16)
    low = (total - high.astype(F32)).astype(BF16)
    weights = proj_ref[0]
    full = (jnp.dot(high, weights, preferred_element_type=F32)
            + jnp.dot(low, weights, preferred_element_type=F32))
    full = jnp.where(lax.broadcasted_iota(jnp.int32, (ROWS, 128), 1) < widths_ref[tab], full, 0.0)
    fsum[...] = full
    for h in range(32):
        hot_all[pl.ds(h, 1), :] = fsum[pl.ds(hot_ref[0, h], 1), :]
    give = remote(hot_all.at[pl.ds(pl.multiple_of((1 - rep) * 16, 16), 16)], hot_got, hot_s, hot_r, {"rep": 1 - rep})
    give.start()
    is_hot = rows == hot_ref[0, 0]
    for h in range(1, 32):
        is_hot = is_hot | (rows == hot_ref[0, h])
    cold_ref[0, 0] = jnp.where(is_hot, 0.0, full)
    give.wait()
    hotout_ref[0] = hot_all[pl.ds(pl.multiple_of(rep * 16, 16), 16), :] + hot_got[...]

    def drain(i, c):
        mode = i % 2
        step = i // 2
        for d in range(1, 4):
            raw_copy(mode, step, d).wait_send()
        for side in range(2):
            leaf_copy(mode, step, side).wait_send()
            near_copy(mode, step, side).wait_send()

        @pl.when(pair_of(step) * 2 + mode - z != 0)
        def _():
            z_copy(mode, step).wait_send()

        return c

    lax.fori_loop(0, 8, drain, 0)


def shards(grad_out, indices, projections, widths, hot_ids):
    z = (lax.axis_index("tab") // NX) % NZ
    by_place = indices.reshape(NY, NZ, NX, 2, 128)
    y_first = by_place.transpose(1, 2, 0, 3, 4).reshape(NZ, 4, 8, 128)
    x_first = by_place.transpose(1, 0, 2, 3, 4).reshape(NZ, 4, 8, 128)
    idx = jnp.where(z % 2 == 0, y_first, x_first)
    vmem = pl.BlockSpec(memory_space=pltpu.VMEM)
    smem = pl.BlockSpec(memory_space=pltpu.SMEM)
    dma = pltpu.SemaphoreType.DMA
    cold, hot = pl.pallas_call(
        kernel,
        out_shape=(jax.ShapeDtypeStruct((1, 1, ROWS, 128), F32), jax.ShapeDtypeStruct((1, 16, 128), F32)),
        in_specs=[pl.BlockSpec(memory_space=pl.ANY), vmem, vmem, smem, smem],
        out_specs=(vmem, vmem),
        scratch_shapes=[
            pltpu.VMEM((4, 4, 256, 8, 128), BF16),
            pltpu.VMEM((2048, 128), F32),
            pltpu.VMEM((2, 4, 4, 4, 256, 128), BF16),
            pltpu.VMEM((2, 4, 3, 4, 256, 128), BF16),
            pltpu.VMEM((ROWS, 128), F32),
            pltpu.VMEM((2, 4, ROWS, 128), F32),
            pltpu.VMEM((2, 4, 3, ROWS, 128), BF16),
            pltpu.VMEM((2, 4, 2, ROWS // 2, 128), BF16),
            pltpu.VMEM((2, 4, 2, ROWS, 128), BF16),
            pltpu.VMEM((2, 4, ROWS, 128), BF16),
            pltpu.VMEM((8, ROWS, 128), BF16),
            pltpu.VMEM((2, 4, 4, 8, 128), jnp.int32),
            pltpu.VMEM((2, 4, 4, 8, 128), jnp.int32),
            pltpu.VMEM((32, 128), F32),
            pltpu.VMEM((16, 128), F32),
            dma((4, 4)), dma((2, 4, 3)), dma((2, 4, 3)), dma((2, 4, 2)), dma((2, 4, 2)),
            dma((2, 4, 2)), dma((2, 4, 2)), dma((2, 4)), dma((8,)),
            dma((7,)), dma((7,)), dma((2, 3)), dma((2, 3)), dma, dma,
        ],
        compiler_params=pltpu.CompilerParams(
            collective_id=0, has_side_effects=True, vmem_limit_bytes=64_000_000),
    )(grad_out, idx, projections, widths, hot_ids)
    return cold, hot


def solution(mesh):
    placed = (
        P(("rep", "tab"), None, None),
        P("tab", "rep"),
        P("tab", None, None),
        P(),
        P("tab", None),
    )
    return jax.shard_map(
        shards,
        mesh=mesh,
        in_specs=placed,
        out_specs=(P("rep", "tab", None, None), P("tab", "rep", None)),
        check_vma=False,
    )
```

time: 288 us -> 139 us (0.48)
  the two profiles are of different devices: /device:TPU:1 before, /device:TPU:2 now
where the time goes in v1:
time: 139 us
  Pallas kernels  133 us (96%)
  local copies, waits for them, and re-layouts  3.16 us (2%)
  other arithmetic  1.71 us (1%)
    pallas_call x1, Pallas kernels, shards(): pl.pallas_call(kernel, out_shape=(jax.ShapeDtypeStruct((1, 1, ROWS, 128),...  133 us
    unnamed x2, local copies, waits for them, and re-layouts  3.16 us

profile of v1, /device:TPU:2, one launch (start us, length us, event | category | flops | bytes accessed | tf_op | source)
XLA Modules:
  0.0 138.8 jit_solution(7782378963562765292)
XLA Ops:
  0.7 1.7 %bitcast_select_fusion = s32[8,4,4,2,128]{4,3,2,1,0:T(2,128)} fusion(s32[4,8,4,2,128]{4,3,2,1,0:T(2,128)} %bitcast.7, pred[]{:T(512)S(6)} %eq.6), kind=kLoop, calls=%fused_computation | loop fusion | flops 32768 | bytes 262145 | tf_op jit(solution)/shard_map/jit(_where)/select_n | solution.py:271
  2.4 133.3 %shard_map.68 = (f32[1,1,1024,128]{3,2,1,0:T(8,128)}, f32[1,16,128]{2,1,0:T(8,128)}) custom-call(bf16[256,128,128]{2,1,0:T(8,128)(2,1)} %grad_ref.1, s32[8,4,8,128]{3,2,1,0:T(8,128)} %bitcast.6, bf16[1,128,128]{2,1,0:T(8,128)(2,1)} %proj_ref.1, s32[128]{0:T(128)} %widths_ref.1, s32[1,32]{1,0:T(1,128)} %hot_ref.1), custom_call_target="tpu_custom_call" | custom-call | tf_op jit(solution)/shard_map/pallas_call | solution.py:275
  135.7 1.9 %copy.13 = f32[1,1,1024,128]{3,2,1,0:T(8,128)} copy(f32[1,1,1024,128]{3,2,1,0:T(8,128)} %get-tuple-element.4) | data formatting | bytes 1048576
  137.5 1.3 copy.14

commit v2 on v1

--- a/solution.py
+++ b/solution.py
@@ -13,7 +13,7 @@
 
 
 def kernel(grad_ref, idx_ref, proj_ref, widths_ref, hot_ref, cold_ref, hotout_ref,
-           stage, tmp, turn, raw, fsum, own, part, leaf, near, zsend, zrecv,
+           stage, tmp, turn, raw, fsum, own, joined, part, leaf, near, zsend, zrecv,
            zi, pi, hot_all, hot_got,
            load_sem, raw_s, raw_r, leaf_s, leaf_r, near_s, near_r, z_s, z_r,
            iz_s, iz_r, iq_s, iq_r, hot_s, hot_r):
@@ -35,14 +35,24 @@
             src_ref=src, dst_ref=dst, send_sem=s, recv_sem=r,
             device_id=dev, device_id_type=pl.DeviceIdType.MESH)
 
-    def pair_of(step):
-        return (z // 2 + 2 + 3 * step + (step // 2) * (3 - 2 * (step % 2))) % 4
-
-    def load(step, d):
-        tile = ((y + d) % NY) * 4 + pair_of(step)
+    def home_of(mode):
+        return (z + mode + 1) % 2
+
+    def offset_of(mode, step):
+        home = 4 - 2 * step + (step // 2) * (6 + 4 * (step % 2))
+        return home_of(mode) * home + (1 - home_of(mode)) * (7 - home)
+
+    def pair_of(mode, step):
+        return ((z + offset_of(mode, step) + 8) % NZ) // 2
+
+    def nth_pair(n):
+        return (z // 2 + 2 + 3 * n + 3 * (n // 2) + 2 * (n // 3) + 4) % 4
+
+    def load(n, d):
+        tile = ((y + d) % NY) * 4 + nth_pair(n)
         return pltpu.make_async_copy(
             grad_ref.at[:, pl.ds(pl.multiple_of(tile * 8, 8), 8), :],
-            stage.at[step, d], load_sem.at[step, d])
+            stage.at[n, d], load_sem.at[n, d])
 
     def start_loads(i, c):
         load(i // 4, i % 4).start()
@@ -73,29 +83,33 @@
 
     def raw_copy(mode, step, d):
         pos = y * (1 - mode) + x * mode
-        return remote(turn.at[mode, step, (pos + d) % 4], raw.at[mode, step, d - 1],
+        return remote(turn.at[mode, pair_of(mode, step), (pos + d) % 4], raw.at[mode, step, d - 1],
                       raw_s.at[mode, step, d - 1], raw_r.at[mode, step, d - 1], peer(mode, 0, d))
 
-    def relayout(step):
-        def one(d, c):
-            load(step, d).wait()
-            tmp[...] = stage[step, d].astype(F32).reshape(2048, 128)
-            to_y = (y + d) % NY
-            for px in range(4):
-                turn[0, step, to_y, px] = tmp[pl.ds(px, 256, stride=8), :].astype(BF16)
-            for px in range(4):
-                turn[1, step, px, to_y] = tmp[pl.ds(4 + px, 256, stride=8), :].astype(BF16)
-            return c
-
-        lax.fori_loop(0, 4, one, 0)
-
+    def relayout(i, c):
+        n = i // 4
+        d = i % 4
+        load(n, d).wait()
+        tmp[...] = stage[n, d].astype(F32).reshape(2048, 128)
+        to_y = (y + d) % NY
+        pair = nth_pair(n)
+        for px in range(4):
+            turn[0, pair, to_y, px] = tmp[pl.ds(px, 256, stride=8), :].astype(BF16)
+        for px in range(4):
+            turn[1, pair, px, to_y] = tmp[pl.ds(4 + px, 256, stride=8), :].astype(BF16)
+        return c
+
+    def send_raw(step):
         def send(i, c):
             raw_copy(i % 2, step, i // 2 + 1).start()
             return c
 
         lax.fori_loop(0, 6, send, 0)
 
-    relayout(0)
+    lax.fori_loop(0, 8, relayout, 0)
+    send_raw(0)
+    lax.fori_loop(8, 16, relayout, 0)
+    send_raw(1)
 
     def iq(mode, d):
         pos = x * (1 - mode) + y * mode
@@ -124,38 +138,30 @@
 
     def table_sum(mode, step, dest):
         pos = y * (1 - mode) + x * mode
-        ids = (mode, pair_of(step), dest)
-        fsum[...] = jnp.dot(onehot(ids, pos), turn[mode, step, pos, dest], preferred_element_type=F32)
-
-        def other(d, c):
-            src = (pos + 4 - d) % 4
-            fsum[...] += jnp.dot(onehot(ids, src), raw[mode, step, d - 1, dest], preferred_element_type=F32)
-            return c
-
-        lax.fori_loop(1, 4, other, 0)
+        pair = pair_of(mode, step)
+        values = jnp.concatenate([turn[mode, pair, pos, dest]] + [raw[mode, step, d - 1, dest] for d in range(1, 4)], axis=0)
+        ones = jnp.concatenate([onehot((mode, pair, dest), (pos + 4 - d) % 4) for d in range(4)], axis=1)
+        fsum[...] = jnp.dot(ones, values, preferred_element_type=F32)
 
     HALF = ROWS // 2
 
+    def half(h):
+        return pl.ds(pl.multiple_of(h * HALF, HALF), HALF)
+
     def leaf_copy(mode, step, side):
-        return remote(part.at[mode, step, 0, pl.ds(side * HALF, HALF)], leaf.at[mode, step, side],
+        return remote(part.at[mode, step, 0, half(side)], leaf.at[mode, step, side],
                       leaf_s.at[mode, step, side], leaf_r.at[mode, step, side], peer(mode, 1, 1 + 2 * side))
 
-    def near_copy(mode, step, side):
-        return remote(part.at[mode, step, 1 + side], near.at[mode, step, side],
-                      near_s.at[mode, step, side], near_r.at[mode, step, side], peer(mode, 1, 1 + 2 * side))
-
-    def z_copy(mode, step):
-        to = pair_of(step) * 2 + mode
-        return remote(zsend.at[mode, step], zrecv.at[z], z_s.at[mode, step], z_r.at[z], at(x, y, to))
-
-    def z_arrival(src):
-        return remote(zsend.at[0, 0], zrecv.at[src], z_s.at[0, 0], z_r.at[src], at(x, y, src))
+    def near_copy(mode, step, side, h):
+        return remote(part.at[mode, step, 1 + side, half(h)], near.at[mode, step, side, half(h)],
+                      near_s.at[mode, step, side, h], near_r.at[mode, step, side, h], peer(mode, 1, 1 + 2 * side))
+
+    def z_copy(mode, step, h):
+        to = (z + 1 + 6 * ((home_of(mode) + step) % 2)) % NZ
+        return remote(zsend.at[mode, step, half(h)], zrecv.at[mode, step, half(h)],
+                      z_s.at[mode, step, h], z_r.at[mode, step, h], at(x, y, to))
 
     def step_body(step, c):
-        @pl.when(step < STEPS - 1)
-        def _():
-            relayout(step + 1)
-
         def arrive(i, c):
             raw_copy(i % 2, step, i // 2 + 1).wait_recv()
             return c
@@ -166,7 +172,7 @@
             mode = i % 2
             j = i // 2
             pos = x * (1 - mode) + y * mode
-            shift = (2 + 2 * j + 3 * (j // 2)) % 4
+            shift = (2 + 3 * j + (j // 2) * (3 - 2 * (j % 2))) % 4
             table_sum(mode, step, (pos + shift) % 4)
 
             @pl.when(j == 0)
@@ -175,22 +181,35 @@
                 leaf_copy(mode, step, 0).start()
                 leaf_copy(mode, step, 1).start()
 
-            @pl.when(j == 1)
-            def _():
-                own[mode, step] = fsum[...]
-
-            @pl.when(j >= 2)
-            def _():
-                side = j - 2
-                leaf_copy(mode, step, side).wait_recv()
-                at_row = pl.multiple_of(side * HALF, HALF)
-                fsum[pl.ds(at_row, HALF), :] += leaf[mode, step, side].astype(F32)
-                part[mode, step, 1 + side] = fsum[...].astype(BF16)
-                near_copy(mode, step, side).start()
+            @pl.when((i == 1) & (step < STEPS - 2))
+            def _():
+                send_raw(step + 2)
+
+            @pl.when((j == 1) | (j == 2))
+            def _():
+                side = j - 1
+                free = half(1 - side)
+                part[mode, step, 1 + side, free] = fsum[free, :].astype(BF16)
+                near_copy(mode, step, side, 1 - side).start()
+                joined[mode, side] = fsum[half(side), :]
+
+            @pl.when(j == 3)
+            def _():
+                own[mode, step % 2] = fsum[...]
 
             return c
 
         lax.fori_loop(0, 8, table, 0)
+
+        def join(i, c):
+            mode = i % 2
+            side = i // 2
+            leaf_copy(mode, step, side).wait_recv()
+            part[mode, step, 1 + side, half(side)] = (joined[mode, side] + leaf[mode, step, side].astype(F32)).astype(BF16)
+            near_copy(mode, step, side, side).start()
+            return c
+
+        lax.fori_loop(0, 4, join, 0)
 
         @pl.when(step > 0)
         def _():
@@ -199,32 +218,35 @@
         return c
 
     def finish(step):
-        def one(mode, c):
-            near_copy(mode, step, 0).wait_recv()
-            near_copy(mode, step, 1).wait_recv()
-            zsend[mode, step] = (own[mode, step] + near[mode, step, 0].astype(F32)
-                                 + near[mode, step, 1].astype(F32)).astype(BF16)
-
-            @pl.when(pair_of(step) * 2 + mode - z != 0)
-            def _():
-                z_copy(mode, step).start()
-
-            return c
-
-        lax.fori_loop(0, 2, one, 0)
+        def one(i, c):
+            mode = (1 + z + i) % 2
+            h = i // 2
+            rows_h = half(h)
+            near_copy(mode, step, 0, h).wait_recv()
+            near_copy(mode, step, 1, h).wait_recv()
+            fsum[rows_h, :] = (own[mode, step % 2, rows_h, :] + near[mode, step, 0, rows_h, :].astype(F32)
+                               + near[mode, step, 1, rows_h, :].astype(F32))
+
+            @pl.when(step > 0)
+            def _():
+                z_copy(mode, step - 1, h).wait_recv()
+                fsum[rows_h, :] += zrecv[mode, step - 1, rows_h, :].astype(F32)
+
+            @pl.when((home_of(mode) == 0) | (step < STEPS - 1))
+            def _():
+                zsend[mode, step, rows_h, :] = fsum[rows_h, :].astype(BF16)
+                z_copy(mode, step, h).start()
+
+            return c
+
+        lax.fori_loop(0, 4, one, 0)
 
     lax.fori_loop(0, STEPS, step_body, 0)
     finish(STEPS - 1)
 
-    fsum[...] = zsend[z % 2, STEPS - 1].astype(F32)
-
-    def gather_z(d, c):
-        src = (z + d) % NZ
-        z_arrival(src).wait_recv()
-        fsum[...] += zrecv[src].astype(F32)
-        return c
-
-    lax.fori_loop(1, 8, gather_z, 0)
+    for h in range(2):
+        z_copy(z % 2, STEPS - 1, h).wait_recv()
+        fsum[half(h), :] += zrecv[z % 2, STEPS - 1, half(h), :].astype(F32)
 
     total = fsum[...]
     high = total.astype(BF16)
@@ -252,11 +274,13 @@
             raw_copy(mode, step, d).wait_send()
         for side in range(2):
             leaf_copy(mode, step, side).wait_send()
-            near_copy(mode, step, side).wait_send()
-
-        @pl.when(pair_of(step) * 2 + mode - z != 0)
+            for h in range(2):
+                near_copy(mode, step, side, h).wait_send()
+
+        @pl.when((home_of(mode) == 0) | (step < STEPS - 1))
         def _():
-            z_copy(mode, step).wait_send()
+            for h in range(2):
+                z_copy(mode, step, h).wait_send()
 
         return c
 
@@ -283,18 +307,19 @@
             pltpu.VMEM((2, 4, 4, 4, 256, 128), BF16),
             pltpu.VMEM((2, 4, 3, 4, 256, 128), BF16),
             pltpu.VMEM((ROWS, 128), F32),
-            pltpu.VMEM((2, 4, ROWS, 128), F32),
+            pltpu.VMEM((2, 2, ROWS, 128), F32),
+            pltpu.VMEM((2, 2, ROWS // 2, 128), F32),
             pltpu.VMEM((2, 4, 3, ROWS, 128), BF16),
             pltpu.VMEM((2, 4, 2, ROWS // 2, 128), BF16),
             pltpu.VMEM((2, 4, 2, ROWS, 128), BF16),
             pltpu.VMEM((2, 4, ROWS, 128), BF16),
-            pltpu.VMEM((8, ROWS, 128), BF16),
+            pltpu.VMEM((2, 4, ROWS, 128), BF16),
             pltpu.VMEM((2, 4, 4, 8, 128), jnp.int32),
             pltpu.VMEM((2, 4, 4, 8, 128), jnp.int32),
             pltpu.VMEM((32, 128), F32),
             pltpu.VMEM((16, 128), F32),
             dma((4, 4)), dma((2, 4, 3)), dma((2, 4, 3)), dma((2, 4, 2)), dma((2, 4, 2)),
-            dma((2, 4, 2)), dma((2, 4, 2)), dma((2, 4)), dma((8,)),
+            dma((2, 4, 2, 2)), dma((2, 4, 2, 2)), dma((2, 4, 2)), dma((2, 4, 2)),
             dma((7,)), dma((7,)), dma((2, 3)), dma((2, 3)), dma, dma,
         ],
         compiler_params=pltpu.CompilerParams(

time: 139 us -> 118 us (0.85)
  the two profiles are of different devices: /device:TPU:2 before, /device:TPU:1 now
where the time goes in v2:
time: 118 us; the launch traced here: 117 us
  Pallas kernels  111 us (94%)
  local copies, waits for them, and re-layouts  3.16 us (3%)
  other arithmetic  1.71 us (1%)
    pallas_call x1, Pallas kernels, shards(): pl.pallas_call(kernel, out_shape=(jax.ShapeDtypeStruct((1, 1, ROWS, 128),...  111 us
    unnamed x2, local copies, waits for them, and re-layouts  3.16 us

profile of v2, /device:TPU:1, one launch (start us, length us, event | category | flops | bytes accessed | tf_op | source)
XLA Modules:
  0.0 116.6 jit_solution(13455725993401364969)
XLA Ops:
  0.7 1.7 %bitcast_select_fusion = s32[8,4,4,2,128]{4,3,2,1,0:T(2,128)} fusion(s32[4,8,4,2,128]{4,3,2,1,0:T(2,128)} %bitcast.7, pred[]{:T(512)S(6)} %eq.6), kind=kLoop, calls=%fused_computation | loop fusion | flops 32768 | bytes 262145 | tf_op jit(solution)/shard_map/jit(_where)/select_n | solution.py:295
  2.4 111.1 %shard_map.68 = (f32[1,1,1024,128]{3,2,1,0:T(8,128)}, f32[1,16,128]{2,1,0:T(8,128)}) custom-call(bf16[256,128,128]{2,1,0:T(8,128)(2,1)} %grad_ref.1, s32[8,4,8,128]{3,2,1,0:T(8,128)} %bitcast.6, bf16[1,128,128]{2,1,0:T(8,128)(2,1)} %proj_ref.1, s32[128]{0:T(128)} %widths_ref.1, s32[1,32]{1,0:T(1,128)} %hot_ref.1), custom_call_target="tpu_custom_call" | custom-call | tf_op jit(solution)/shard_map/pallas_call | solution.py:299
  113.5 1.9 %copy.13 = f32[1,1,1024,128]{3,2,1,0:T(8,128)} copy(f32[1,1,1024,128]{3,2,1,0:T(8,128)} %get-tuple-element.4) | data formatting | bytes 1048576
  115.3 1.3 %copy.14 = f32[1,16,128]{2,1,0:T(8,128)} copy(f32[1,16,128]{2,1,0:T(8,128)} %get-tuple-element.5) | data formatting | bytes 16384

commit v3 on v2

--- a/solution.py
+++ b/solution.py
@@ -12,11 +12,11 @@
 BF16 = jnp.bfloat16
 
 
-def kernel(grad_ref, idx_ref, proj_ref, widths_ref, hot_ref, cold_ref, hotout_ref,
+def kernel(grad_ref, idx_ref, hot_ref, sums_ref, hotsum_ref,
            stage, tmp, turn, raw, fsum, own, joined, part, leaf, near, zsend, zrecv,
            zi, pi, hot_all, hot_got,
            load_sem, raw_s, raw_r, leaf_s, leaf_r, near_s, near_r, z_s, z_r,
-           iz_s, iz_r, iq_s, iq_r, hot_s, hot_r):
+           iz_s, iz_r, iq_s, iq_r, hot_s, hot_r, own_sem, round_a, round_b):
     rep = lax.axis_index("rep")
     tab = lax.axis_index("tab")
     x = tab % NX
@@ -68,18 +68,10 @@
     for d in range(1, 4):
         greet(at((x + d) % NX, y, z))
         greet(at(x, (y + d) % NY, z))
-    for d in range(1, 8):
+    for d in (1, 7):
         greet(at(x, y, (z + d) % NZ))
     greet({"rep": 1 - rep})
-    pl.semaphore_wait(barrier, 14)
-
-    def iz(d):
-        to = (z + d) % NZ
-        return remote(idx_ref.at[to], zi.at[z % 2, z // 2], iz_s.at[d - 1], iz_r.at[d - 1], at(x, y, to))
-
-    for d in range(1, 8):
-        iz(d).start()
-    zi[z % 2, z // 2] = idx_ref[z]
+    pl.semaphore_wait(barrier, 9)
 
     def raw_copy(mode, step, d):
         pos = y * (1 - mode) + x * mode
@@ -108,12 +100,27 @@
 
     lax.fori_loop(0, 8, relayout, 0)
     send_raw(0)
+
+    for sem, away in ((round_a, 1), (round_b, 2)):
+        for d in (away, 8 - away):
+            pl.semaphore_signal(sem, inc=1, device_id=at(x, y, (z + d) % NZ), device_id_type=pl.DeviceIdType.MESH)
+        pl.semaphore_wait(sem, 2)
+
+    def iz(d):
+        to = (z + d) % NZ
+        return remote(idx_ref.at[:, to], zi.at[z % 2, z // 2], iz_s.at[d - 1], iz_r.at[d - 1], at(x, y, to))
+
+    for d in range(1, 8):
+        iz(d).start()
+    own_idx = pltpu.make_async_copy(idx_ref.at[:, z], zi.at[z % 2, z // 2], own_sem)
+    own_idx.start()
     lax.fori_loop(8, 16, relayout, 0)
-    send_raw(1)
+    own_idx.wait()
 
     def iq(mode, d):
         pos = x * (1 - mode) + y * mode
-        return remote(zi.at[mode, :, (pos + d) % 4], pi.at[mode, :, pos],
+        to = (pos + d) % 4
+        return remote(zi.at[0, :, :, to] if mode == 0 else zi.at[1, :, to], pi.at[mode, :, pos],
                       iq_s.at[mode, d - 1], iq_r.at[mode, d - 1], peer(mode, 1, d))
 
     for d in range(1, 8):
@@ -121,7 +128,8 @@
     for mode in range(2):
         for d in range(1, 4):
             iq(mode, d).start()
-    pi[0, :, x] = zi[0, :, x]
+    send_raw(1)
+    pi[0, :, x] = zi[0, :, :, x]
     pi[1, :, y] = zi[1, :, y]
     for mode in range(2):
         for d in range(1, 4):
@@ -132,7 +140,7 @@
     def onehot(ids, src):
         halves = []
         for h in range(2):
-            line = pi[ids + (pl.ds(2 * src + h, 1), slice(None))]
+            line = pi[ids + (src, pl.ds(h, 1), slice(None))]
             halves.append(jnp.where(rows == line, F32(1), F32(0)).astype(BF16))
         return jnp.concatenate(halves, axis=1)
 
@@ -246,26 +254,12 @@
 
     for h in range(2):
         z_copy(z % 2, STEPS - 1, h).wait_recv()
-        fsum[half(h), :] += zrecv[z % 2, STEPS - 1, half(h), :].astype(F32)
-
-    total = fsum[...]
-    high = total.astype(BF16)
-    low = (total - high.astype(F32)).astype(BF16)
-    weights = proj_ref[0]
-    full = (jnp.dot(high, weights, preferred_element_type=F32)
-            + jnp.dot(low, weights, preferred_element_type=F32))
-    full = jnp.where(lax.broadcasted_iota(jnp.int32, (ROWS, 128), 1) < widths_ref[tab], full, 0.0)
-    fsum[...] = full
+        sums_ref[half(h), :] = fsum[half(h), :] + zrecv[z % 2, STEPS - 1, half(h), :].astype(F32)
+
     for h in range(32):
-        hot_all[pl.ds(h, 1), :] = fsum[pl.ds(hot_ref[0, h], 1), :]
+        hot_all[pl.ds(h, 1), :] = sums_ref[pl.ds(hot_ref[0, h], 1), :]
     give = remote(hot_all.at[pl.ds(pl.multiple_of((1 - rep) * 16, 16), 16)], hot_got, hot_s, hot_r, {"rep": 1 - rep})
     give.start()
-    is_hot = rows == hot_ref[0, 0]
-    for h in range(1, 32):
-        is_hot = is_hot | (rows == hot_ref[0, h])
-    cold_ref[0, 0] = jnp.where(is_hot, 0.0, full)
-    give.wait()
-    hotout_ref[0] = hot_all[pl.ds(pl.multiple_of(rep * 16, 16), 16), :] + hot_got[...]
 
     def drain(i, c):
         mode = i % 2
@@ -285,21 +279,38 @@
         return c
 
     lax.fori_loop(0, 8, drain, 0)
+    give.wait()
+    hotsum_ref[...] = hot_all[pl.ds(pl.multiple_of(rep * 16, 16), 16), :] + hot_got[...]
+
+
+def outputs(sums_ref, hotsum_ref, proj_ref, widths_ref, hot_ref, cold_ref, hotout_ref):
+    width = widths_ref[lax.axis_index("tab")]
+    weights = proj_ref[0]
+
+    def project(total):
+        high = total.astype(BF16)
+        low = (total - high.astype(F32)).astype(BF16)
+        full = (jnp.dot(high, weights, preferred_element_type=F32)
+                + jnp.dot(low, weights, preferred_element_type=F32))
+        return jnp.where(lax.broadcasted_iota(jnp.int32, full.shape, 1) < width, full, 0.0)
+
+    rows = lax.broadcasted_iota(jnp.int32, (ROWS, 128), 0)
+    is_hot = rows == hot_ref[0, 0]
+    for h in range(1, 32):
+        is_hot = is_hot | (rows == hot_ref[0, h])
+    cold_ref[0, 0] = jnp.where(is_hot, 0.0, project(sums_ref[...]))
+    hotout_ref[0] = project(hotsum_ref[...])
 
 
 def shards(grad_out, indices, projections, widths, hot_ids):
-    z = (lax.axis_index("tab") // NX) % NZ
-    by_place = indices.reshape(NY, NZ, NX, 2, 128)
-    y_first = by_place.transpose(1, 2, 0, 3, 4).reshape(NZ, 4, 8, 128)
-    x_first = by_place.transpose(1, 0, 2, 3, 4).reshape(NZ, 4, 8, 128)
-    idx = jnp.where(z % 2 == 0, y_first, x_first)
+    idx = indices.reshape(NY, NZ, NX, 2, 128)
     vmem = pl.BlockSpec(memory_space=pltpu.VMEM)
     smem = pl.BlockSpec(memory_space=pltpu.SMEM)
     dma = pltpu.SemaphoreType.DMA
-    cold, hot = pl.pallas_call(
+    sums, hot_sums = pl.pallas_call(
         kernel,
-        out_shape=(jax.ShapeDtypeStruct((1, 1, ROWS, 128), F32), jax.ShapeDtypeStruct((1, 16, 128), F32)),
-        in_specs=[pl.BlockSpec(memory_space=pl.ANY), vmem, vmem, smem, smem],
+        out_shape=(jax.ShapeDtypeStruct((ROWS, 128), F32), jax.ShapeDtypeStruct((16, 128), F32)),
+        in_specs=[pl.BlockSpec(memory_space=pl.ANY), pl.BlockSpec(memory_space=pl.ANY), smem],
         out_specs=(vmem, vmem),
         scratch_shapes=[
             pltpu.VMEM((4, 4, 256, 8, 128), BF16),
@@ -314,18 +325,24 @@
             pltpu.VMEM((2, 4, 2, ROWS, 128), BF16),
             pltpu.VMEM((2, 4, ROWS, 128), BF16),
             pltpu.VMEM((2, 4, ROWS, 128), BF16),
-            pltpu.VMEM((2, 4, 4, 8, 128), jnp.int32),
-            pltpu.VMEM((2, 4, 4, 8, 128), jnp.int32),
+            pltpu.VMEM((2, 4, 4, 4, 2, 128), jnp.int32),
+            pltpu.VMEM((2, 4, 4, 4, 2, 128), jnp.int32),
             pltpu.VMEM((32, 128), F32),
             pltpu.VMEM((16, 128), F32),
             dma((4, 4)), dma((2, 4, 3)), dma((2, 4, 3)), dma((2, 4, 2)), dma((2, 4, 2)),
             dma((2, 4, 2, 2)), dma((2, 4, 2, 2)), dma((2, 4, 2)), dma((2, 4, 2)),
-            dma((7,)), dma((7,)), dma((2, 3)), dma((2, 3)), dma, dma,
+            dma((7,)), dma((7,)), dma((2, 3)), dma((2, 3)), dma, dma, dma,
+            pltpu.SemaphoreType.REGULAR, pltpu.SemaphoreType.REGULAR,
         ],
         compiler_params=pltpu.CompilerParams(
             collective_id=0, has_side_effects=True, vmem_limit_bytes=64_000_000),
-    )(grad_out, idx, projections, widths, hot_ids)
-    return cold, hot
+    )(grad_out, idx, hot_ids)
+    return pl.pallas_call(
+        outputs,
+        out_shape=(jax.ShapeDtypeStruct((1, 1, ROWS, 128), F32), jax.ShapeDtypeStruct((1, 16, 128), F32)),
+        in_specs=[vmem, vmem, vmem, smem, smem],
+        out_specs=(vmem, vmem),
+    )(sums, hot_sums, projections, widths, hot_ids)
 
 
 def solution(mesh):

time: 118 us -> 108 us (0.915)
  Pallas kernels: 111 us -> 107 us
  local copies, waits for them, and re-layouts: 3.16 us -> 0 us
  other arithmetic: 1.71 us -> 0 us
    pallas_call x1 -> x2, Pallas kernels: 111 us -> 107 us  [the longest x1 103 us: shards(): pl.pallas_call(kernel, out_shape=(jax.ShapeDtypeStruct((ROWS, 128), F32),...]
    unnamed x2 -> x0, local copies, waits for them, and re-layouts: 3.16 us -> none
    select_n x1 -> x0, other arithmetic: 1.71 us -> none  [shards(): idx = jnp.where(z % 2 == 0, y_first, x_first)]
where the time goes in v3:
time: 108 us
  Pallas kernels  107 us (99%)
    pallas_call x1, Pallas kernels, shards(): pl.pallas_call(kernel, out_shape=(jax.ShapeDtypeStruct((ROWS, 128), F32),...  103 us
    pallas_call x1, Pallas kernels, shards(): pl.pallas_call(outputs, out_shape=(jax.ShapeDtypeStruct((1, 1, ROWS, 128)...  4.08 us

profile of v3, /device:TPU:1, one launch (start us, length us, event | category | flops | bytes accessed | tf_op | source)
XLA Modules:
  0.0 107.5 jit_solution(8964425985946401016)
XLA Ops:
  0.6 102.8 %shard_map.68 = (f32[1024,128]{1,0:T(8,128)}, f32[16,128]{1,0:T(8,128)}) custom-call(bf16[256,128,128]{2,1,0:T(8,128)(2,1)} %grad_ref.1, s32[4,8,4,2,128]{4,3,2,1,0:T(2,128)} %bitcast.1, s32[1,32]{1,0:T(1,128)} %hot_ref.3), custom_call_target="tpu_custom_call" | custom-call | tf_op jit(solution)/shard_map/pallas_call | solution.py:310
  103.4 4.1 %shard_map.69 = (f32[1,1,1024,128]{3,2,1,0:T(8,128)}, f32[1,16,128]{2,1,0:T(8,128)}) custom-call(f32[1024,128]{1,0:T(8,128)} %get-tuple-element.4.sums_ref, f32[16,128]{1,0:T(8,128)} %get-tuple-element.5.hotsum_ref, bf16[1,128,128]{2,1,0:T(8,128)(2,1)} %proj_ref.1, s32[128]{0:T(128)} %widths_ref.1, s32[1,32]{1,0:T(1,128)} %hot_ref.3), custom_call_target="tpu_custom_call" | custom-call | tf_op jit(solution)/shard_map/pallas_call | solution.py:340

commit v4 on v3

--- a/solution.py
+++ b/solution.py
@@ -8,14 +8,15 @@
 ROWS = 1024
 NX, NY, NZ = 4, 4, 8
 STEPS = 4
+PRE = 1
 F32 = jnp.float32
 BF16 = jnp.bfloat16
 
 
 def kernel(grad_ref, idx_ref, hot_ref, sums_ref, hotsum_ref,
-           stage, tmp, turn, raw, fsum, own, joined, part, leaf, near, zsend, zrecv,
+           stage, tmp, turn, raw, fsum, own, joined, part, leaf, near, zsend, zrecv, early, before,
            zi, pi, hot_all, hot_got,
-           load_sem, raw_s, raw_r, leaf_s, leaf_r, near_s, near_r, z_s, z_r,
+           load_sem, raw_s, raw_r, leaf_s, leaf_r, near_s, near_r, z_s, z_r, early_s, early_r,
            iz_s, iz_r, iq_s, iq_r, hot_s, hot_r, own_sem, round_a, round_b):
     rep = lax.axis_index("rep")
     tab = lax.axis_index("tab")
@@ -157,17 +158,23 @@
         return pl.ds(pl.multiple_of(h * HALF, HALF), HALF)
 
     def leaf_copy(mode, step, side):
-        return remote(part.at[mode, step, 0, half(side)], leaf.at[mode, step, side],
-                      leaf_s.at[mode, step, side], leaf_r.at[mode, step, side], peer(mode, 1, 1 + 2 * side))
+        return remote(part.at[mode, step - PRE, 0, half(side)], leaf.at[mode, step - PRE, side],
+                      leaf_s.at[mode, step - PRE, side], leaf_r.at[mode, step - PRE, side], peer(mode, 1, 1 + 2 * side))
 
     def near_copy(mode, step, side, h):
-        return remote(part.at[mode, step, 1 + side, half(h)], near.at[mode, step, side, half(h)],
-                      near_s.at[mode, step, side, h], near_r.at[mode, step, side, h], peer(mode, 1, 1 + 2 * side))
+        return remote(part.at[mode, step - PRE, 1 + side, half(h)], near.at[mode, step - PRE, side, half(h)],
+                      near_s.at[mode, step - PRE, side, h], near_r.at[mode, step - PRE, side, h], peer(mode, 1, 1 + 2 * side))
+
+    def along_z(mode, step):
+        return at(x, y, (z + 1 + 6 * ((home_of(mode) + step) % 2)) % NZ)
 
     def z_copy(mode, step, h):
-        to = (z + 1 + 6 * ((home_of(mode) + step) % 2)) % NZ
-        return remote(zsend.at[mode, step, half(h)], zrecv.at[mode, step, half(h)],
-                      z_s.at[mode, step, h], z_r.at[mode, step, h], at(x, y, to))
+        return remote(zsend.at[mode, step - PRE, half(h)], zrecv.at[mode, step - PRE, half(h)],
+                      z_s.at[mode, step - PRE, h], z_r.at[mode, step - PRE, h], along_z(mode, step))
+
+    def early_copy(mode, step, dest):
+        return remote(early.at[mode, step, dest], before.at[mode, step, dest],
+                      early_s.at[mode, step, dest], early_r.at[mode, step, dest], along_z(mode, step))
 
     def step_body(step, c):
         def arrive(i, c):
@@ -181,11 +188,22 @@
             j = i // 2
             pos = x * (1 - mode) + y * mode
             shift = (2 + 3 * j + (j // 2) * (3 - 2 * (j % 2))) % 4
-            table_sum(mode, step, (pos + shift) % 4)
-
-            @pl.when(j == 0)
-            def _():
-                part[mode, step, 0] = fsum[...].astype(BF16)
+            dest = (pos + shift) % 4
+            table_sum(mode, step, dest)
+
+            @pl.when((step >= 1) & (step <= PRE))
+            def _():
+                early_copy(mode, step - 1, dest).wait_recv()
+                fsum[...] += before[mode, step - 1, dest].astype(F32)
+
+            @pl.when(step < PRE)
+            def _():
+                early[mode, step, dest] = fsum[...].astype(BF16)
+                early_copy(mode, step, dest).start()
+
+            @pl.when((j == 0) & (step >= PRE))
+            def _():
+                part[mode, step - PRE, 0] = fsum[...].astype(BF16)
                 leaf_copy(mode, step, 0).start()
                 leaf_copy(mode, step, 1).start()
 
@@ -193,15 +211,15 @@
             def _():
                 send_raw(step + 2)
 
-            @pl.when((j == 1) | (j == 2))
+            @pl.when(((j == 1) | (j == 2)) & (step >= PRE))
             def _():
                 side = j - 1
                 free = half(1 - side)
-                part[mode, step, 1 + side, free] = fsum[free, :].astype(BF16)
+                part[mode, step - PRE, 1 + side, free] = fsum[free, :].astype(BF16)
                 near_copy(mode, step, side, 1 - side).start()
                 joined[mode, side] = fsum[half(side), :]
 
-            @pl.when(j == 3)
+            @pl.when((j == 3) & (step >= PRE))
             def _():
                 own[mode, step % 2] = fsum[...]
 
@@ -213,13 +231,15 @@
             mode = i % 2
             side = i // 2
             leaf_copy(mode, step, side).wait_recv()
-            part[mode, step, 1 + side, half(side)] = (joined[mode, side] + leaf[mode, step, side].astype(F32)).astype(BF16)
+            part[mode, step - PRE, 1 + side, half(side)] = (joined[mode, side] + leaf[mode, step - PRE, side].astype(F32)).astype(BF16)
             near_copy(mode, step, side, side).start()
             return c
 
-        lax.fori_loop(0, 4, join, 0)
-
-        @pl.when(step > 0)
+        @pl.when(step >= PRE)
+        def _():
+            lax.fori_loop(0, 4, join, 0)
+
+        @pl.when(step > PRE)
         def _():
             finish(step - 1)
 
@@ -232,17 +252,17 @@
             rows_h = half(h)
             near_copy(mode, step, 0, h).wait_recv()
             near_copy(mode, step, 1, h).wait_recv()
-            fsum[rows_h, :] = (own[mode, step % 2, rows_h, :] + near[mode, step, 0, rows_h, :].astype(F32)
-                               + near[mode, step, 1, rows_h, :].astype(F32))
-
-            @pl.when(step > 0)
+            fsum[rows_h, :] = (own[mode, step % 2, rows_h, :] + near[mode, step - PRE, 0, rows_h, :].astype(F32)
+                               + near[mode, step - PRE, 1, rows_h, :].astype(F32))
+
+            @pl.when(step > PRE)
             def _():
                 z_copy(mode, step - 1, h).wait_recv()
-                fsum[rows_h, :] += zrecv[mode, step - 1, rows_h, :].astype(F32)
+                fsum[rows_h, :] += zrecv[mode, step - 1 - PRE, rows_h, :].astype(F32)
 
             @pl.when((home_of(mode) == 0) | (step < STEPS - 1))
             def _():
-                zsend[mode, step, rows_h, :] = fsum[rows_h, :].astype(BF16)
+                zsend[mode, step - PRE, rows_h, :] = fsum[rows_h, :].astype(BF16)
                 z_copy(mode, step, h).start()
 
             return c
@@ -254,7 +274,7 @@
 
     for h in range(2):
         z_copy(z % 2, STEPS - 1, h).wait_recv()
-        sums_ref[half(h), :] = fsum[half(h), :] + zrecv[z % 2, STEPS - 1, half(h), :].astype(F32)
+        sums_ref[half(h), :] = fsum[half(h), :] + zrecv[z % 2, STEPS - 1 - PRE, half(h), :].astype(F32)
 
     for h in range(32):
         hot_all[pl.ds(h, 1), :] = sums_ref[pl.ds(hot_ref[0, h], 1), :]
@@ -266,12 +286,20 @@
         step = i // 2
         for d in range(1, 4):
             raw_copy(mode, step, d).wait_send()
-        for side in range(2):
-            leaf_copy(mode, step, side).wait_send()
-            for h in range(2):
-                near_copy(mode, step, side, h).wait_send()
-
-        @pl.when((home_of(mode) == 0) | (step < STEPS - 1))
+
+        @pl.when(step < PRE)
+        def _():
+            for dest in range(4):
+                early_copy(mode, step, dest).wait_send()
+
+        @pl.when(step >= PRE)
+        def _():
+            for side in range(2):
+                leaf_copy(mode, step, side).wait_send()
+                for h in range(2):
+                    near_copy(mode, step, side, h).wait_send()
+
+        @pl.when((step >= PRE) & ((home_of(mode) == 0) | (step < STEPS - 1)))
         def _():
             for h in range(2):
                 z_copy(mode, step, h).wait_send()
@@ -294,11 +322,9 @@
                 + jnp.dot(low, weights, preferred_element_type=F32))
         return jnp.where(lax.broadcasted_iota(jnp.int32, full.shape, 1) < width, full, 0.0)
 
-    rows = lax.broadcasted_iota(jnp.int32, (ROWS, 128), 0)
-    is_hot = rows == hot_ref[0, 0]
-    for h in range(1, 32):
-        is_hot = is_hot | (rows == hot_ref[0, h])
-    cold_ref[0, 0] = jnp.where(is_hot, 0.0, project(sums_ref[...]))
+    cold_ref[0, 0] = project(sums_ref[...])
+    for h in range(32):
+        cold_ref[0, 0, pl.ds(hot_ref[0, h], 1), :] = jnp.zeros((1, 128), F32)
     hotout_ref[0] = project(hotsum_ref[...])
 
 
@@ -320,17 +346,20 @@
             pltpu.VMEM((ROWS, 128), F32),
             pltpu.VMEM((2, 2, ROWS, 128), F32),
             pltpu.VMEM((2, 2, ROWS // 2, 128), F32),
-            pltpu.VMEM((2, 4, 3, ROWS, 128), BF16),
-            pltpu.VMEM((2, 4, 2, ROWS // 2, 128), BF16),
-            pltpu.VMEM((2, 4, 2, ROWS, 128), BF16),
-            pltpu.VMEM((2, 4, ROWS, 128), BF16),
-            pltpu.VMEM((2, 4, ROWS, 128), BF16),
+            pltpu.VMEM((2, STEPS - PRE, 3, ROWS, 128), BF16),
+            pltpu.VMEM((2, STEPS - PRE, 2, ROWS // 2, 128), BF16),
+            pltpu.VMEM((2, STEPS - PRE, 2, ROWS, 128), BF16),
+            pltpu.VMEM((2, STEPS - PRE, ROWS, 128), BF16),
+            pltpu.VMEM((2, STEPS - PRE, ROWS, 128), BF16),
+            pltpu.VMEM((2, PRE, 4, ROWS, 128), BF16),
+            pltpu.VMEM((2, PRE, 4, ROWS, 128), BF16),
             pltpu.VMEM((2, 4, 4, 4, 2, 128), jnp.int32),
             pltpu.VMEM((2, 4, 4, 4, 2, 128), jnp.int32),
             pltpu.VMEM((32, 128), F32),
             pltpu.VMEM((16, 128), F32),
             dma((4, 4)), dma((2, 4, 3)), dma((2, 4, 3)), dma((2, 4, 2)), dma((2, 4, 2)),
             dma((2, 4, 2, 2)), dma((2, 4, 2, 2)), dma((2, 4, 2)), dma((2, 4, 2)),
+            dma((2, PRE, 4)), dma((2, PRE, 4)),
             dma((7,)), dma((7,)), dma((2, 3)), dma((2, 3)), dma, dma, dma,
             pltpu.SemaphoreType.REGULAR, pltpu.SemaphoreType.REGULAR,
         ],

time: 108 us -> 97.8 us (0.906)
  Pallas kernels: 107 us -> 96.7 us
    pallas_call x1, Pallas kernels: 103 us -> 94.5 us  [shards(): pl.pallas_call(kernel, out_shape=(jax.ShapeDtypeStruct((ROWS, 128), F32),...]
    pallas_call x1, Pallas kernels: 4.08 us -> 2.19 us  [shards(): pl.pallas_call(outputs, out_shape=(jax.ShapeDtypeStruct((1, 1, ROWS, 128)...]
where the time goes in v4:
time: 97.8 us; the launch traced here: 97.3 us
  Pallas kernels  96.7 us (99%)
    pallas_call x1, Pallas kernels, shards(): pl.pallas_call(kernel, out_shape=(jax.ShapeDtypeStruct((ROWS, 128), F32),...  94.5 us
    pallas_call x1, Pallas kernels, shards(): pl.pallas_call(outputs, out_shape=(jax.ShapeDtypeStruct((1, 1, ROWS, 128)...  2.19 us

profile of v4, /device:TPU:1, one launch (start us, length us, event | category | flops | bytes accessed | tf_op | source)
XLA Modules:
  0.0 97.3 jit_solution(16284667669411685428)
XLA Ops:
  0.6 94.5 %shard_map.68 = (f32[1024,128]{1,0:T(8,128)}, f32[16,128]{1,0:T(8,128)}) custom-call(bf16[256,128,128]{2,1,0:T(8,128)(2,1)} %grad_ref.1, s32[4,8,4,2,128]{4,3,2,1,0:T(2,128)} %bitcast.1, s32[1,32]{1,0:T(1,128)} %hot_ref.3), custom_call_target="tpu_custom_call" | custom-call | tf_op jit(solution)/shard_map/pallas_call | solution.py:336
  95.1 2.2 %shard_map.69 = (f32[1,1,1024,128]{3,2,1,0:T(8,128)}, f32[1,16,128]{2,1,0:T(8,128)}) custom-call(f32[1024,128]{1,0:T(8,128)} %get-tuple-element.4.sums_ref, f32[16,128]{1,0:T(8,128)} %get-tuple-element.5.hotsum_ref, bf16[1,128,128]{2,1,0:T(8,128)(2,1)} %proj_ref.1, s32[128]{0:T(128)} %widths_ref.1, s32[1,32]{1,0:T(1,128)} %hot_ref.3), custom_call_target="tpu_custom_call" | custom-call | tf_op jit(solution)/shard_map/pallas_call | solution.py:369

commit v5 on v4

--- a/solution.py
+++ b/solution.py
@@ -8,13 +8,14 @@
 ROWS = 1024
 NX, NY, NZ = 4, 4, 8
 STEPS = 4
+PIECE = 256
 PRE = 1
 F32 = jnp.float32
 BF16 = jnp.bfloat16
 
 
 def kernel(grad_ref, idx_ref, hot_ref, sums_ref, hotsum_ref,
-           stage, tmp, turn, raw, fsum, own, joined, part, leaf, near, zsend, zrecv, early, before,
+           stage, tmp, turn, raw, fsum, own, joined, far, part, leaf, near, zsend, zrecv, early, before,
            zi, pi, hot_all, hot_got,
            load_sem, raw_s, raw_r, leaf_s, leaf_r, near_s, near_r, z_s, z_r, early_s, early_r,
            iz_s, iz_r, iq_s, iq_r, hot_s, hot_r, own_sem, round_a, round_b):
@@ -59,7 +60,7 @@
         load(i // 4, i % 4).start()
         return c
 
-    lax.fori_loop(0, 16, start_loads, 0)
+    lax.fori_loop(0, 8, start_loads, 0)
 
     barrier = pltpu.get_barrier_semaphore()
 
@@ -73,6 +74,7 @@
         greet(at(x, y, (z + d) % NZ))
     greet({"rep": 1 - rep})
     pl.semaphore_wait(barrier, 9)
+    lax.fori_loop(8, 16, start_loads, 0)
 
     def raw_copy(mode, step, d):
         pos = y * (1 - mode) + x * mode
@@ -157,20 +159,23 @@
     def half(h):
         return pl.ds(pl.multiple_of(h * HALF, HALF), HALF)
 
-    def leaf_copy(mode, step, side):
-        return remote(part.at[mode, step - PRE, 0, half(side)], leaf.at[mode, step - PRE, side],
-                      leaf_s.at[mode, step - PRE, side], leaf_r.at[mode, step - PRE, side], peer(mode, 1, 1 + 2 * side))
-
-    def near_copy(mode, step, side, h):
-        return remote(part.at[mode, step - PRE, 1 + side, half(h)], near.at[mode, step - PRE, side, half(h)],
-                      near_s.at[mode, step - PRE, side, h], near_r.at[mode, step - PRE, side, h], peer(mode, 1, 1 + 2 * side))
+    def piece(p):
+        return pl.ds(pl.multiple_of(p * PIECE, PIECE), PIECE)
+
+    def leaf_copy(mode, side, p):
+        return remote(far.at[mode, piece(2 * side + p)], leaf.at[mode, piece(2 * side + p)],
+                      leaf_s.at[mode, side, p], leaf_r.at[mode, side, p], peer(mode, 1, 1 + 2 * side))
+
+    def near_copy(mode, step, side, p):
+        return remote(part.at[mode, step - PRE, side, piece(p)], near.at[mode, step - PRE, side, piece(p)],
+                      near_s.at[mode, step - PRE, side, p], near_r.at[mode, step - PRE, side, p], peer(mode, 1, 1 + 2 * side))
 
     def along_z(mode, step):
         return at(x, y, (z + 1 + 6 * ((home_of(mode) + step) % 2)) % NZ)
 
-    def z_copy(mode, step, h):
-        return remote(zsend.at[mode, step - PRE, half(h)], zrecv.at[mode, step - PRE, half(h)],
-                      z_s.at[mode, step - PRE, h], z_r.at[mode, step - PRE, h], along_z(mode, step))
+    def z_copy(mode, step, p):
+        return remote(zsend.at[mode, step - PRE, piece(p)], zrecv.at[mode, step - PRE, piece(p)],
+                      z_s.at[mode, step - PRE, p], z_r.at[mode, step - PRE, p], along_z(mode, step))
 
     def early_copy(mode, step, dest):
         return remote(early.at[mode, step, dest], before.at[mode, step, dest],
@@ -185,38 +190,46 @@
 
         def table(i, c):
             mode = i % 2
-            j = i // 2
+            j = (i // 2 + (step // 2) * (1 - step % 2)) % 4
             pos = x * (1 - mode) + y * mode
             shift = (2 + 3 * j + (j // 2) * (3 - 2 * (j % 2))) % 4
             dest = (pos + shift) % 4
             table_sum(mode, step, dest)
 
-            @pl.when((step >= 1) & (step <= PRE))
+            @pl.when((step >= 1) & ((step <= PRE) | (j == 0)))
             def _():
                 early_copy(mode, step - 1, dest).wait_recv()
                 fsum[...] += before[mode, step - 1, dest].astype(F32)
 
-            @pl.when(step < PRE)
+            @pl.when((step < PRE) | ((j == 0) & (step < STEPS - 1)))
             def _():
                 early[mode, step, dest] = fsum[...].astype(BF16)
                 early_copy(mode, step, dest).start()
 
-            @pl.when((j == 0) & (step >= PRE))
-            def _():
-                part[mode, step - PRE, 0] = fsum[...].astype(BF16)
-                leaf_copy(mode, step, 0).start()
-                leaf_copy(mode, step, 1).start()
+            @pl.when((j == 0) & (step == STEPS - 1))
+            def _():
+                far[mode] = fsum[...].astype(BF16)
+                for p in range(2):
+                    leaf_copy(mode, 0, p).start()
+                    leaf_copy(mode, 1, p).start()
 
             @pl.when((i == 1) & (step < STEPS - 2))
             def _():
                 send_raw(step + 2)
 
-            @pl.when(((j == 1) | (j == 2)) & (step >= PRE))
+            @pl.when(((j == 1) | (j == 2)) & (step >= PRE) & (step < STEPS - 1))
+            def _():
+                part[mode, step - PRE, j - 1] = fsum[...].astype(BF16)
+                for p in range(4):
+                    near_copy(mode, step, j - 1, p).start()
+
+            @pl.when(((j == 1) | (j == 2)) & (step == STEPS - 1))
             def _():
                 side = j - 1
                 free = half(1 - side)
-                part[mode, step - PRE, 1 + side, free] = fsum[free, :].astype(BF16)
-                near_copy(mode, step, side, 1 - side).start()
+                part[mode, step - PRE, side, free] = fsum[free, :].astype(BF16)
+                for p in range(2):
+                    near_copy(mode, step, side, 2 * (1 - side) + p).start()
                 joined[mode, side] = fsum[half(side), :]
 
             @pl.when((j == 3) & (step >= PRE))
@@ -227,54 +240,54 @@
 
         lax.fori_loop(0, 8, table, 0)
 
-        def join(i, c):
-            mode = i % 2
-            side = i // 2
-            leaf_copy(mode, step, side).wait_recv()
-            part[mode, step - PRE, 1 + side, half(side)] = (joined[mode, side] + leaf[mode, step - PRE, side].astype(F32)).astype(BF16)
-            near_copy(mode, step, side, side).start()
-            return c
-
-        @pl.when(step >= PRE)
-        def _():
-            lax.fori_loop(0, 4, join, 0)
-
         @pl.when(step > PRE)
         def _():
             finish(step - 1)
 
+        return c
+
+    def join(i, c):
+        mode = i % 2
+        side = (i // 2) % 2
+        p = i // 4
+        at_piece = piece(2 * side + p)
+        leaf_copy(mode, side, p).wait_recv()
+        part[mode, STEPS - 1 - PRE, side, at_piece] = (
+            joined[mode, side, piece(p)] + leaf[mode, at_piece].astype(F32)).astype(BF16)
+        near_copy(mode, STEPS - 1, side, 2 * side + p).start()
         return c
 
     def finish(step):
         def one(i, c):
             mode = (1 + z + i) % 2
-            h = i // 2
-            rows_h = half(h)
-            near_copy(mode, step, 0, h).wait_recv()
-            near_copy(mode, step, 1, h).wait_recv()
-            fsum[rows_h, :] = (own[mode, step % 2, rows_h, :] + near[mode, step - PRE, 0, rows_h, :].astype(F32)
-                               + near[mode, step - PRE, 1, rows_h, :].astype(F32))
+            p = (i // 2) // 2 + 2 * ((i // 2) % 2)
+            rows_p = piece(p)
+            near_copy(mode, step, 0, p).wait_recv()
+            near_copy(mode, step, 1, p).wait_recv()
+            fsum[rows_p, :] = (own[mode, step % 2, rows_p, :] + near[mode, step - PRE, 0, rows_p, :].astype(F32)
+                               + near[mode, step - PRE, 1, rows_p, :].astype(F32))
 
             @pl.when(step > PRE)
             def _():
-                z_copy(mode, step - 1, h).wait_recv()
-                fsum[rows_h, :] += zrecv[mode, step - 1 - PRE, rows_h, :].astype(F32)
+                z_copy(mode, step - 1, p).wait_recv()
+                fsum[rows_p, :] += zrecv[mode, step - 1 - PRE, rows_p, :].astype(F32)
 
             @pl.when((home_of(mode) == 0) | (step < STEPS - 1))
             def _():
-                zsend[mode, step - PRE, rows_h, :] = fsum[rows_h, :].astype(BF16)
-                z_copy(mode, step, h).start()
+                zsend[mode, step - PRE, rows_p, :] = fsum[rows_p, :].astype(BF16)
+                z_copy(mode, step, p).start()
 
             return c
 
-        lax.fori_loop(0, 4, one, 0)
+        lax.fori_loop(0, 8, one, 0)
 
     lax.fori_loop(0, STEPS, step_body, 0)
+    lax.fori_loop(0, 8, join, 0)
     finish(STEPS - 1)
 
-    for h in range(2):
-        z_copy(z % 2, STEPS - 1, h).wait_recv()
-        sums_ref[half(h), :] = fsum[half(h), :] + zrecv[z % 2, STEPS - 1 - PRE, half(h), :].astype(F32)
+    for p in (0, 2, 1, 3):
+        z_copy(z % 2, STEPS - 1, p).wait_recv()
+        sums_ref[piece(p), :] = fsum[piece(p), :] + zrecv[z % 2, STEPS - 1 - PRE, piece(p), :].astype(F32)
 
     for h in range(32):
         hot_all[pl.ds(h, 1), :] = sums_ref[pl.ds(hot_ref[0, h], 1), :]
@@ -292,17 +305,27 @@
             for dest in range(4):
                 early_copy(mode, step, dest).wait_send()
 
+        @pl.when((step >= PRE) & (step < STEPS - 1))
+        def _():
+            pos = x * (1 - mode) + y * mode
+            early_copy(mode, step, (pos + 2) % 4).wait_send()
+
         @pl.when(step >= PRE)
         def _():
             for side in range(2):
-                leaf_copy(mode, step, side).wait_send()
-                for h in range(2):
-                    near_copy(mode, step, side, h).wait_send()
+                for p in range(4):
+                    near_copy(mode, step, side, p).wait_send()
+
+        @pl.when(step == STEPS - 1)
+        def _():
+            for side in range(2):
+                for p in range(2):
+                    leaf_copy(mode, side, p).wait_send()
 
         @pl.when((step >= PRE) & ((home_of(mode) == 0) | (step < STEPS - 1)))
         def _():
-            for h in range(2):
-                z_copy(mode, step, h).wait_send()
+            for p in range(4):
+                z_copy(mode, step, p).wait_send()
 
         return c
 
@@ -346,20 +369,21 @@
             pltpu.VMEM((ROWS, 128), F32),
             pltpu.VMEM((2, 2, ROWS, 128), F32),
             pltpu.VMEM((2, 2, ROWS // 2, 128), F32),
-            pltpu.VMEM((2, STEPS - PRE, 3, ROWS, 128), BF16),
-            pltpu.VMEM((2, STEPS - PRE, 2, ROWS // 2, 128), BF16),
+            pltpu.VMEM((2, ROWS, 128), BF16),
+            pltpu.VMEM((2, STEPS - PRE, 2, ROWS, 128), BF16),
+            pltpu.VMEM((2, ROWS, 128), BF16),
             pltpu.VMEM((2, STEPS - PRE, 2, ROWS, 128), BF16),
             pltpu.VMEM((2, STEPS - PRE, ROWS, 128), BF16),
             pltpu.VMEM((2, STEPS - PRE, ROWS, 128), BF16),
-            pltpu.VMEM((2, PRE, 4, ROWS, 128), BF16),
-            pltpu.VMEM((2, PRE, 4, ROWS, 128), BF16),
+            pltpu.VMEM((2, STEPS - 1, 4, ROWS, 128), BF16),
+            pltpu.VMEM((2, STEPS - 1, 4, ROWS, 128), BF16),
             pltpu.VMEM((2, 4, 4, 4, 2, 128), jnp.int32),
             pltpu.VMEM((2, 4, 4, 4, 2, 128), jnp.int32),
             pltpu.VMEM((32, 128), F32),
             pltpu.VMEM((16, 128), F32),
-            dma((4, 4)), dma((2, 4, 3)), dma((2, 4, 3)), dma((2, 4, 2)), dma((2, 4, 2)),
-            dma((2, 4, 2, 2)), dma((2, 4, 2, 2)), dma((2, 4, 2)), dma((2, 4, 2)),
-            dma((2, PRE, 4)), dma((2, PRE, 4)),
+            dma((4, 4)), dma((2, 4, 3)), dma((2, 4, 3)), dma((2, 2, 2)), dma((2, 2, 2)),
+            dma((2, STEPS - PRE, 2, 4)), dma((2, STEPS - PRE, 2, 4)), dma((2, STEPS - PRE, 4)), dma((2, STEPS - PRE, 4)),
+            dma((2, STEPS - 1, 4)), dma((2, STEPS - 1, 4)),
             dma((7,)), dma((7,)), dma((2, 3)), dma((2, 3)), dma, dma, dma,
             pltpu.SemaphoreType.REGULAR, pltpu.SemaphoreType.REGULAR,
         ],

time: 97.8 us -> 93.4 us (0.955)
  Pallas kernels: 96.7 us -> 92.7 us
    pallas_call x1, Pallas kernels: 94.5 us -> 90.5 us  [shards(): pl.pallas_call(kernel, out_shape=(jax.ShapeDtypeStruct((ROWS, 128), F32),...]
where the time goes in v5:
time: 93.4 us; the launch traced here: 93.3 us
  Pallas kernels  92.7 us (99%)
    pallas_call x1, Pallas kernels, shards(): pl.pallas_call(kernel, out_shape=(jax.ShapeDtypeStruct((ROWS, 128), F32),...  90.5 us
    pallas_call x1, Pallas kernels, shards(): pl.pallas_call(outputs, out_shape=(jax.ShapeDtypeStruct((1, 1, ROWS, 128)...  2.19 us

profile of v5, /device:TPU:1, one launch (start us, length us, event | category | flops | bytes accessed | tf_op | source)
XLA Modules:
  0.0 93.3 jit_solution(8997451213927043634)
XLA Ops:
  0.6 90.5 %shard_map.68 = (f32[1024,128]{1,0:T(8,128)}, f32[16,128]{1,0:T(8,128)}) custom-call(bf16[256,128,128]{2,1,0:T(8,128)(2,1)} %grad_ref.1, s32[4,8,4,2,128]{4,3,2,1,0:T(2,128)} %bitcast.1, s32[1,32]{1,0:T(1,128)} %hot_ref.3), custom_call_target="tpu_custom_call" | custom-call | tf_op jit(solution)/shard_map/pallas_call | solution.py:359
  91.1 2.2 %shard_map.69 = (f32[1,1,1024,128]{3,2,1,0:T(8,128)}, f32[1,16,128]{2,1,0:T(8,128)}) custom-call(f32[1024,128]{1,0:T(8,128)} %get-tuple-element.4.sums_ref, f32[16,128]{1,0:T(8,128)} %get-tuple-element.5.hotsum_ref, bf16[1,128,128]{2,1,0:T(8,128)(2,1)} %proj_ref.1, s32[128]{0:T(128)} %widths_ref.1, s32[1,32]{1,0:T(1,128)} %hot_ref.3), custom_call_target="tpu_custom_call" | custom-call | tf_op jit(solution)/shard_map/pallas_call | solution.py:393

commit v6 on v5

--- a/solution.py
+++ b/solution.py
@@ -213,7 +213,7 @@
                     leaf_copy(mode, 0, p).start()
                     leaf_copy(mode, 1, p).start()
 
-            @pl.when((i == 1) & (step < STEPS - 2))
+            @pl.when((i == 1 + 4 * step) & (step < STEPS - 2))
             def _():
                 send_raw(step + 2)
 

time: 93.4 us -> 92.6 us (level)
  no operation moved by 1% of the time
where the time goes in v6:
time: 92.6 us; the launch traced here: 92.4 us
  Pallas kernels  91.8 us (99%)
    pallas_call x1, Pallas kernels, shards(): pl.pallas_call(kernel, out_shape=(jax.ShapeDtypeStruct((ROWS, 128), F32),...  89.6 us
    pallas_call x1, Pallas kernels, shards(): pl.pallas_call(outputs, out_shape=(jax.ShapeDtypeStruct((1, 1, ROWS, 128)...  2.19 us

profile of v6, /device:TPU:1, one launch (start us, length us, event | category | flops | bytes accessed | tf_op | source)
XLA Modules:
  0.0 92.4 jit_solution(11677806693251058983)
XLA Ops:
  0.6 89.6 %shard_map.68 = (f32[1024,128]{1,0:T(8,128)}, f32[16,128]{1,0:T(8,128)}) custom-call(bf16[256,128,128]{2,1,0:T(8,128)(2,1)} %grad_ref.1, s32[4,8,4,2,128]{4,3,2,1,0:T(2,128)} %bitcast.1, s32[1,32]{1,0:T(1,128)} %hot_ref.3), custom_call_target="tpu_custom_call" | custom-call | tf_op jit(solution)/shard_map/pallas_call | solution.py:359
  90.2 2.2 %shard_map.69 = (f32[1,1,1024,128]{3,2,1,0:T(8,128)}, f32[1,16,128]{2,1,0:T(8,128)}) custom-call(f32[1024,128]{1,0:T(8,128)} %get-tuple-element.4.sums_ref, f32[16,128]{1,0:T(8,128)} %get-tuple-element.5.hotsum_ref, bf16[1,128,128]{2,1,0:T(8,128)(2,1)} %proj_ref.1, s32[128]{0:T(128)} %widths_ref.1, s32[1,32]{1,0:T(1,128)} %hot_ref.3), custom_call_target="tpu_custom_call" | custom-call | tf_op jit(solution)/shard_map/pallas_call | solution.py:393

commit v7 on v6

--- a/solution.py
+++ b/solution.py
@@ -358,7 +358,7 @@
     dma = pltpu.SemaphoreType.DMA
     sums, hot_sums = pl.pallas_call(
         kernel,
-        out_shape=(jax.ShapeDtypeStruct((ROWS, 128), F32), jax.ShapeDtypeStruct((16, 128), F32)),
+        out_shape=(pltpu.VMEM((ROWS, 128), F32), pltpu.VMEM((16, 128), F32)),
         in_specs=[pl.BlockSpec(memory_space=pl.ANY), pl.BlockSpec(memory_space=pl.ANY), smem],
         out_specs=(vmem, vmem),
         scratch_shapes=[
@@ -388,13 +388,14 @@
             pltpu.SemaphoreType.REGULAR, pltpu.SemaphoreType.REGULAR,
         ],
         compiler_params=pltpu.CompilerParams(
-            collective_id=0, has_side_effects=True, vmem_limit_bytes=64_000_000),
+            collective_id=0, has_side_effects=True, vmem_limit_bytes=60_000_000),
     )(grad_out, idx, hot_ids)
     return pl.pallas_call(
         outputs,
         out_shape=(jax.ShapeDtypeStruct((1, 1, ROWS, 128), F32), jax.ShapeDtypeStruct((1, 16, 128), F32)),
         in_specs=[vmem, vmem, vmem, smem, smem],
         out_specs=(vmem, vmem),
+        compiler_params=pltpu.CompilerParams(vmem_limit_bytes=8_000_000),
     )(sums, hot_sums, projections, widths, hot_ids)
 
 

time: 92.6 us -> 91.4 us (0.987)
  Pallas kernels: 91.8 us -> 90.5 us
where the time goes in v7:
time: 91.4 us; the launch traced here: 91.2 us
  Pallas kernels  90.5 us (99%)
    pallas_call x1, Pallas kernels, shards(): pl.pallas_call(kernel, out_shape=(pltpu.VMEM((ROWS, 128), F32), pltpu.VME...  88.8 us

profile of v7, /device:TPU:1, one launch (start us, length us, event | category | flops | bytes accessed | tf_op | source)
XLA Modules:
  0.0 91.2 jit_solution(11598253451672106031)
XLA Ops:
  0.6 0.0 copy-start.1
  0.6 0.0 copy-start.2
  0.7 0.0 copy-start
  0.7 88.8 %shard_map.68 = (f32[1024,128]{1,0:T(8,128)S(1)}, f32[16,128]{1,0:T(8,128)S(1)}) custom-call(bf16[256,128,128]{2,1,0:T(8,128)(2,1)} %grad_ref.1, s32[4,8,4,2,128]{4,3,2,1,0:T(2,128)} %bitcast.1, s32[1,32]{1,0:T(1,128)} %hot_ref.3), custom_call_target="tpu_custom_call" | custom-call | tf_op jit(solution)/shard_map/pallas_call | solution.py:359
  89.5 0.0 copy-done.1
  89.5 0.0 copy-done.2
  89.5 0.0 copy-done
  89.5 1.7 %shard_map.69 = (f32[1,1,1024,128]{3,2,1,0:T(8,128)}, f32[1,16,128]{2,1,0:T(8,128)}) custom-call(f32[1024,128]{1,0:T(8,128)S(1)} %get-tuple-element.4.sums_ref, f32[16,128]{1,0:T(8,128)S(1)} %get-tuple-element.5.hotsum_ref, bf16[1,128,128]{2,1,0:T(8,128)(2,1)S(1)} %copy-done, s32[128]{0:T(128)S(1)} %copy-done.2, s32[1,32]{1,0:T(1,128)S(1)} %copy-done.1), custom_call_target="tpu_custom_call" | custom-call | tf_op jit(solution)/shard_map/pallas_call | solution.py:393
Async XLA Ops:
  0.6 88.9 %copy-start.1 = (s32[1,32]{1,0:T(1,128)S(1)}, s32[1,32]{1,0:T(1,128)}, u32[]{:S(2)}) copy-start(s32[1,32]{1,0:T(1,128)} %hot_ref.3) | copy-start | bytes 388
  0.6 88.9 %copy-start.2 = (s32[128]{0:T(128)S(1)}, s32[128]{0:T(128)}, u32[]{:S(2)}) copy-start(s32[128]{0:T(128)} %widths_ref.1) | copy-start | bytes 1540
  0.7 88.9 %copy-start = (bf16[1,128,128]{2,1,0:T(8,128)(2,1)S(1)}, bf16[1,128,128]{2,1,0:T(8,128)(2,1)}, u32[]{:S(2)}) copy-start(bf16[1,128,128]{2,1,0:T(8,128)(2,1)} %proj_ref.1) | copy-start | bytes 98308
